TPU v7x, 32 devices: a 4x4x1 block of a 4x4x8 slice. The times are simulated.
32 devices in a mesh: replica: 1 (over z), data2: 4 (over y), data: 8 (over x, core).
Axes of the slice: x: 4, y: 4, z: 1, core: 2. Of those that a mesh axis runs over, the one named last changes fastest.
The devices are a block of a 4x4x8 slice.
Arguments:
- query_hidden: bfloat16 [256, 32, 1024], P(('replica', 'data2', 'data'))
- doc_hidden: bfloat16 [256, 512, 1024], P(('replica', 'data2', 'data'))
- w_proj: bfloat16 [1024, 128], replicated
- query_mask: int32 [256, 32], P(('replica', 'data2', 'data'))
- doc_mask: int32 [256, 512], P(('replica', 'data2', 'data'))
- temperature: float32 [], replicated
Outputs:
- output 1: float32 [256], P(('replica', 'data2', 'data'))
- output 2: float32 [1], P('replica')
All inputs are finite; a program needn't handle non-finite values.
Results may differ from a plain program's by a relative error of at most 0.001.
Values are sent between devices in bfloat16 or wider.
A program may use at most 768 MiB of HBM per device.

v0:
```python
import jax
import jax.numpy as jnp
from jax import lax
from jax.sharding import PartitionSpec as P


def project_norm(hidden, w_proj):
    projected = jnp.einsum('bld,de->ble', hidden, w_proj, preferred_element_type=jnp.float32)
    norm_len = jnp.sqrt(jnp.sum(projected * projected, axis=-1, keepdims=True))
    return (projected / jnp.maximum(norm_len, 1e-12)).astype(jnp.bfloat16)


def tile_scores(q_block, p_block, doc_valid):
    similarity = jnp.einsum('qtc,jsc->qtjs', q_block, p_block, preferred_element_type=jnp.float32)
    best_match = jnp.max(jnp.where(doc_valid[None, None], similarity, -jnp.inf), axis=-1)
    return jnp.sum(best_match, axis=1)


def solution(mesh):
    outer_size = mesh.shape['data2']
    inner_size = mesh.shape['data']
    group_size = outer_size * inner_size
    batch_axes = ('data2', 'data')
    row_spec = P(('replica', 'data2', 'data'))
    tok_spec = P(('replica', 'data2', 'data'), None, None)
    mask_spec = P(('replica', 'data2', 'data'), None)

    def local_step(query_hidden, doc_hidden, w_proj, query_mask, doc_mask, value_a11):
        local_batch = query_hidden.shape[0]
        total_batch = local_batch * group_size
        q_vecs = project_norm(query_hidden, w_proj)
        q_vecs = jnp.where(query_mask[:, :, None] > 0, q_vecs, jnp.zeros_like(q_vecs))
        p_vecs = project_norm(doc_hidden, w_proj)
        doc_valid = doc_mask > 0
        q_all = lax.all_gather(q_vecs, 'data', axis=0, tiled=True)
        q_all = lax.all_gather(q_all, 'data2', axis=0, tiled=True)
        q_blocks = q_all.reshape(group_size, local_batch, q_all.shape[1], q_all.shape[2])
        column = lax.map(lambda q_block: tile_scores(q_block, p_vecs, doc_valid), q_blocks)
        column = column.reshape(outer_size, inner_size, local_batch, local_batch)
        column = lax.all_to_all(column, 'data', 1, 1, tiled=True)
        column = lax.all_to_all(column, 'data2', 0, 0, tiled=True)
        score_row = jnp.transpose(column, (2, 0, 1, 3)).reshape(local_batch, total_batch)
        logits = score_row / value_a11
        home_index = lax.axis_index('data2') * inner_size + lax.axis_index('data')
        own_logits = lax.dynamic_slice_in_dim(logits, home_index * local_batch, local_batch, axis=1)
        losses = jax.nn.logsumexp(logits, axis=1) - jnp.diagonal(own_logits)
        mean_loss = lax.psum(jnp.sum(losses), batch_axes) / total_batch
        return losses, mean_loss.reshape(1)

    return jax.shard_map(local_step, mesh=mesh, in_specs=(tok_spec, tok_spec, P(None, None), mask_spec, mask_spec, P()), out_specs=(row_spec, P('replica')), check_vma=False)
```

profile of v0, /device:TPU:97, one launch (start us, length us, event | category | flops | bytes accessed | tf_op | source)
XLA Modules:
  0.0 195.0 jit_solution(15392515586396324513)
XLA Ops:
  7.3 1.0 copy-done
  8.2 1.3 multiply_reduce_fusion.1
  9.5 0.7 broadcast_compare_fusion.1
  10.2 0.1 fusion.8
  10.4 19.6 %all_gather.6 = bf16[64,32,128]{2,1,0:T(8,128)(2,1)} all-gather(bf16[8,32,128]{2,1,0:T(8,128)(2,1)S(1)} %fusion.8), channel_id=1, replica_groups=mesh['replica'=1,'data2'=4,'data'=8] {'data'}, dimensions={0}, use_global_device_ids=true | all-gather | bytes 589824 | tf_op jit(solution)/shard_map/all_gather | solution.py:35
  30.0 6.3 %multiply_reduce_fusion = (f32[8,512]{1,0:T(8,128)S(1)}, f32[8,512,128]{1,2,0:T(8,128)S(1)}) fusion(bf16[8,512,1024]{2,1,0:T(8,128)(2,1)} %param.9, bf16[1024,128]{1,0:T(8,128)(2,1)S(1)} %copy-done.1), kind=kOutput, calls=%fused_computation.8 | convolution fusion | flops 1074786304 | bytes 10764288 | tf_op jit(solution)/shard_map/bld,de->ble/dot_general | solution.py:8
  36.4 0.3 divide_convert_fusion
  36.7 0.7 copy.18
  37.4 27.4 %all-gather.2.cloned.1.call-done = bf16[256,32,128]{2,1,0:T(8,128)(2,1)} async-done(((bf16[64,32,128]{2,1,0:T(8,128)(2,1)}), bf16[256,32,128]{2,1,0:T(8,128)(2,1)}) %all-gather.2.cloned.1.call-update) | async-done | bytes 2097168 | tf_op jit(solution)/shard_map/all_gather | solution.py:36
  64.7 55.2 %while.10 = (s32[]{:T(128)}, f32[32,8,8]{2,1,0:T(8,128)S(1)}, pred[8,512]{1,0:T(8,128)(4,1)S(1)}, bf16[32,8,32,128]{3,2,1,0:T(8,128)(2,1)}, bf16[8,512,128]{2,1,0:T(8,128)(2,1)S(1)}, /*index=5*/s32[]{:T(128)}, f32[]{:T(128)}) while((s32[]{:T(128)}, f32[32,8,8]{2,1,0:T(8,128)S(1)}, pred[8,512]{1,0:T(8,128)(4,1)S(1)}, ...), condition=%wide.region_5.6_spmd, body=%wide.region_2.5_spmd.sunk | while | flops 270532544 | bytes 1143637 | solution.py:38
  64.7 1.6 select_reduce_fusion.2
  66.4 0.1 reduce_sum.54
  66.5 1.6 select_reduce_fusion.2
  68.1 0.1 reduce_sum.54
  68.2 1.6 select_reduce_fusion.2
  69.8 0.1 reduce_sum.54
  69.9 1.6 select_reduce_fusion.2
  71.5 0.1 reduce_sum.54
  71.6 1.6 select_reduce_fusion.2
  73.3 0.1 reduce_sum.54
  73.4 1.6 select_reduce_fusion.2
  75.1 1.6 select_reduce_fusion.2
  76.8 1.6 select_reduce_fusion.2
  78.5 1.6 select_reduce_fusion.2
  80.3 1.6 select_reduce_fusion.2
  82.0 1.6 select_reduce_fusion.2
  83.7 1.6 select_reduce_fusion.2
  85.4 1.6 select_reduce_fusion.2
  87.2 1.6 select_reduce_fusion.2
  88.9 1.6 select_reduce_fusion.2
  90.6 1.6 select_reduce_fusion.2
  92.3 1.6 select_reduce_fusion.2
  94.1 1.6 select_reduce_fusion.2
  95.8 1.6 select_reduce_fusion.2
  97.5 1.6 select_reduce_fusion.2
  99.3 1.6 select_reduce_fusion.2
  101.0 1.6 select_reduce_fusion.2
  102.7 1.6 select_reduce_fusion.2
  104.4 1.6 select_reduce_fusion.2
  106.2 1.6 select_reduce_fusion.2
  107.9 1.6 select_reduce_fusion.2
  109.6 1.6 select_reduce_fusion.2
  111.3 1.6 select_reduce_fusion.2
  113.1 1.6 select_reduce_fusion.2
  114.8 1.6 select_reduce_fusion.2
  116.5 1.6 select_reduce_fusion.2
  118.2 1.6 select_reduce_fusion.2
  120.0 0.1 copy.30
  120.1 0.2 reshape.53
  120.2 9.6 %all_to_all.10 = f32[8,1,256]{2,1,0:T(1,128)S(1)} all-to-all(f32[8,1,256]{2,1,0:T(1,128)S(1)} %reshape.53), channel_id=1, replica_groups=mesh['replica'=1,'data2'=4,'data'=8] {'data'}, dimensions={0} | all-to-all | bytes 16384 | tf_op jit(solution)/shard_map/all_to_all | solution.py:40
  129.9 0.5 broadcast.60
  130.4 0.7 reduce.4
  131.0 0.2 reshape.54
  131.3 0.7 reshape.55
  132.0 3.3 %all-to-all-start.1 = ((f32[4,1,512]{2,1,0:T(1,128)}), f32[4,1,512]{2,1,0:T(1,128)S(1)}, u32[]{:S(2)}, u32[]{:S(2)}) async-start(f32[4,1,512]{2,1,0:T(1,128)} %reshape.55), calls=%async_computation.1 | async-start | bytes 16384 | tf_op jit(solution)/shard_map/all_to_all | solution.py:41
  136.0 3.2 %all-to-all-done.1 = f32[4,1,512]{2,1,0:T(1,128)S(1)} async-done(((f32[4,1,512]{2,1,0:T(1,128)}), f32[4,1,512]{2,1,0:T(1,128)S(1)}, u32[]{:S(2)}, u32[]{:S(2)}) %all-to-all-start.1) | async-done | bytes 8224 | tf_op jit(solution)/shard_map/all_to_all | solution.py:41
  139.2 0.7 reduce.5
  139.9 0.1 reshape.56
  140.0 0.2 fusion.10
  140.2 0.2 exponential_reduce_fusion
  140.4 0.1 div.41
  140.6 0.6 gather_fusion
  141.3 1.1 fusion.11
  142.4 44.0 %psum.7 = f32[]{:T(128)} all-reduce(f32[]{:T(128)} %get-tuple-element.60), channel_id=1, replica_groups=mesh['replica'=1,'data2'=4,'data'=8] {'data2','data'}, use_global_device_ids=true, to_apply=%region_9.10 | all-reduce | flops 1 | bytes 8 | tf_op jit(solution)/shard_map/psum | solution.py:47
  (75 shorter events, 2.8 us)
Async XLA Ops:
  7.2 1.0 copy-start
  7.2 22.8 %copy-start.1 = (bf16[1024,128]{1,0:T(8,128)(2,1)S(1)}, bf16[1024,128]{1,0:T(8,128)(2,1)}, u32[]{:S(2)}) copy-start(bf16[1024,128]{1,0:T(8,128)(2,1)} %param.10) | copy-start | bytes 786436
  7.2 57.5 %all-gather.2.cloned.1.call-start = ((), (), s32[]{:S(2)}) async-start(), calls=%async_computation.2 | async-start | bytes 2621440 | tf_op jit(solution)/shard_map/all_gather | solution.py:36
  36.3 1.0 copy-start.2
  132.0 7.2 %all-to-all-start.1 = ((f32[4,1,512]{2,1,0:T(1,128)}), f32[4,1,512]{2,1,0:T(1,128)S(1)}, u32[]{:S(2)}, u32[]{:S(2)}) async-start(f32[4,1,512]{2,1,0:T(1,128)} %reshape.55), calls=%async_computation.1 | async-start | bytes 16384 | tf_op jit(solution)/shard_map/all_to_all | solution.py:41
Sparse Core Ops, SparseCore 0:
  30.1 34.5 all-gather.1
where the time goes:
time: 197 us; the launch traced here: 195 us
  blocking collectives  73.2 us (37%)
  matrix products  59.7 us (30%)
  waiting for transfers between devices  30.6 us (16%)
  between operations  16.7 us (8%)
  other arithmetic  6.69 us (3%)
  local copies, waits for them, and re-layouts  4.49 us (2%)
  starting transfers between devices  3.4 us (2%)
    dot_general x32, matrix products, tile_scores(): jnp.einsum('qtc,jsc->qtjs', q_block, p_block, preferred_element_type=jnp....  52.2 us
    psum x1, blocking collectives, local_step(): mean_loss = lax.psum(jnp.sum(losses), batch_axes) / total_batch  44 us
    all_gather x1, waiting for transfers between devices, local_step(): q_all = lax.all_gather(q_all, 'data2', axis=0, tiled=True)  27.4 us
    all_gather x1, blocking collectives, local_step(): q_all = lax.all_gather(q_vecs, 'data', axis=0, tiled=True)  19.6 us
    all_to_all x1, blocking collectives, local_step(): column = lax.all_to_all(column, 'data', 1, 1, tiled=True)  9.62 us
    dot_general x2, matrix products, project_norm(): jnp.einsum('bld,de->ble', hidden, w_proj, preferred_element_type=jnp.floa...  7.58 us
  transfers between devices with their start and end apart: 2, of which 2 were waited for; matrix products, arithmetic and copies ran while one was open for 4% of the time, Pallas kernels for 0%

commit v1 on v0

v1 whole, which is shorter than its diff:
```python
import functools

import jax
import jax.numpy as jnp
from jax import lax
from jax.experimental import pallas as pl
from jax.experimental.pallas import tpu as pltpu
from jax.sharding import PartitionSpec as P

MESH = pl.DeviceIdType.MESH
CORES = 2
LANES = 128
MASKED = -1e30
DOC_CHUNKS = 4


def unit_rows(hidden, w_proj):
    projected = jnp.dot(hidden, w_proj, preferred_element_type=jnp.float32)
    square = jnp.sum(projected * projected, axis=-1, keepdims=True)
    return projected * lax.rsqrt(jnp.maximum(square, 1e-24))


def kernel(outer, inner, pairs, qlen, dlen,
           hq_hbm, doc_hbm, w_hbm, qm_hbm, dm_hbm, temp_ref, loss_ref, mean_ref,
           hq, doc, w, qm, dm, qall, paug, best, xout, xin,
           load_sem, doc_sem, send_sem, relay_sem, recv_sem, xsend_sem, xrecv_sem):
    devices = outer * inner
    columns = inner // CORES
    chips = outer * columns
    tokens = pairs * qlen
    width = w.shape[1]
    rows = doc.shape[0] // DOC_CHUNKS
    per_half = LANES // pairs
    halves = devices // per_half
    y, d = lax.axis_index('data2'), lax.axis_index('data')
    x, core = d // CORES, d % CORES
    me = y * inner + d
    partner = {'data2': y, 'data': x * CORES + 1 - core}

    loads = [pltpu.make_async_copy(src, dst, load_sem.at[k])
             for k, (src, dst) in enumerate(((w_hbm, w), (hq_hbm, hq), (qm_hbm, qm), (dm_hbm, dm)))]
    for load in loads:
        load.start()
    doc_loads = []
    for k in range(DOC_CHUNKS):
        part = pl.ds(k * rows, rows)
        doc_loads.append(pltpu.make_async_copy(doc_hbm.at[part], doc.at[part], doc_sem.at[k]))
        doc_loads[-1].start()

    barrier = pltpu.get_barrier_semaphore()
    for k in range(1, devices):
        there = {'data2': (y + k // inner) % outer, 'data': (d + k % inner) % inner}
        pl.semaphore_signal(barrier, inc=1, device_id=there, device_id_type=MESH)

    ones = (lax.broadcasted_iota(jnp.int32, (width, tokens), 0) < pairs).astype(jnp.float32).astype(jnp.bfloat16)

    @pl.loop(0, devices)
    def _(slot):
        qall[slot, width:, :] = ones

    loads[3].wait()
    bias = jnp.where(dm[...] > 0, 0.0, MASKED)
    bias = jnp.concatenate([bias, jnp.zeros((LANES - pairs, dlen), jnp.float32)], axis=0).T
    lane = lax.broadcasted_iota(jnp.int32, (dlen, LANES), 1)
    for j in range(pairs):
        paug[j * dlen:(j + 1) * dlen, width:] = jnp.where(lane == j, bias, 0.0).astype(jnp.bfloat16)

    for load in loads[:3]:
        load.wait()
    spread = (lax.broadcasted_iota(jnp.int32, (qlen, tokens), 1) % qlen
              == lax.broadcasted_iota(jnp.int32, (qlen, tokens), 0)).astype(jnp.float32).astype(jnp.bfloat16)
    keep = jnp.dot(qm[...].astype(jnp.float32).astype(jnp.bfloat16), spread, preferred_element_type=jnp.float32)
    own = (lax.broadcasted_iota(jnp.int32, (pairs, tokens), 1) // qlen
           == lax.broadcasted_iota(jnp.int32, (pairs, tokens), 0))
    keep = jnp.sum(jnp.where(own, keep, 0.0), axis=0, keepdims=True)
    q_t = unit_rows(hq[...], w[...]).T
    qall[me, :width, :] = jnp.where(keep > 0, q_t, 0.0).astype(jnp.bfloat16)

    def source(i, other):
        row = (y + outer - i // columns) % outer
        column = (x + columns - i % columns) % columns
        return row * inner + column * CORES + (1 - core if other else core)

    def block_copy(slot, sem, there):
        block = qall.at[slot, pl.ds(0, width), :]
        return pltpu.make_async_remote_copy(
            src_ref=block, dst_ref=block, send_sem=sem, recv_sem=recv_sem.at[slot],
            device_id=there, device_id_type=MESH)

    pl.semaphore_wait(barrier, devices - 1)
    sends = [block_copy(me, relay_sem.at[0], partner)]
    for i in range(1, chips):
        there = {'data2': (y + i // columns) % outer, 'data': (x + i % columns) % columns * CORES + core}
        sends.append(block_copy(me, send_sem.at[i], there))
    for send in sends:
        send.start()

    for k in range(DOC_CHUNKS):
        doc_loads[k].wait()
        part = pl.ds(k * rows, rows)
        paug[part, :width] = unit_rows(doc[part, :], w[...]).astype(jnp.bfloat16)

    def score(slot):
        for j in range(pairs):
            similarity = jnp.dot(paug[j * dlen:(j + 1) * dlen, :], qall[slot], preferred_element_type=jnp.float32)
            similarity = jnp.max(similarity.reshape(4, dlen // 32, 8, tokens), axis=1)
            best[slot, j:j + 1, :] = jnp.max(jnp.max(similarity, axis=0), axis=0, keepdims=True)

    @pl.loop(0, chips)
    def _(i):
        @pl.when(i + 1 < chips)
        def _():
            arrived = source(i + 1, False)
            block_copy(arrived, relay_sem.at[i + 1], partner).wait_recv()
            block_copy(arrived, relay_sem.at[i + 1], partner).start()

        relayed = source(i, True)
        block_copy(relayed, relay_sem.at[i], partner).wait_recv()
        score(source(i, False))
        score(relayed)

    pick = (lax.broadcasted_iota(jnp.int32, (tokens, LANES), 0) // qlen
            == lax.broadcasted_iota(jnp.int32, (tokens, LANES), 1) % pairs).astype(jnp.float32).astype(jnp.bfloat16)
    rest = best[...].reshape(devices * pairs, tokens)
    sums = jnp.zeros((devices * pairs, LANES), jnp.float32)
    for _ in range(3):
        part = rest.astype(jnp.bfloat16)
        sums += jnp.dot(part, pick, preferred_element_type=jnp.float32)
        rest = rest - part.astype(jnp.float32)
    sums = sums.reshape(devices, pairs, LANES)
    lane = lax.broadcasted_iota(jnp.int32, (pairs, LANES), 1)
    own_doc = lane % pairs == lax.broadcasted_iota(jnp.int32, (pairs, LANES), 0)
    temperature = temp_ref[0]
    own_row = jnp.zeros((1, LANES), jnp.float32)
    for h in range(halves):
        logits = jnp.zeros((pairs, LANES), jnp.float32)
        for b in range(per_half):
            logits = jnp.where(lane // pairs == b, sums[h * per_half + b], logits)
        logits = logits / temperature
        top = jnp.max(logits, axis=0, keepdims=True)
        xout[h:h + 1, :] = top + jnp.log(jnp.sum(jnp.exp(logits - top), axis=0, keepdims=True))
        mine = own_doc & (h * per_half + lane // pairs == me)
        own_row += jnp.sum(jnp.where(mine, logits, 0.0), axis=0, keepdims=True)
    xout[halves:halves + 1, :] = own_row
    for h in range(halves + 1, xout.shape[0]):
        xout[h:h + 1, :] = jnp.zeros((1, LANES), jnp.float32)
    xin[me] = xout[...]

    shares = []
    for k in range(1, devices):
        there = {'data2': (y + k // inner) % outer, 'data': (d + k % inner) % inner}
        shares.append(pltpu.make_async_remote_copy(
            src_ref=xout, dst_ref=xin.at[me], send_sem=xsend_sem.at[k], recv_sem=xrecv_sem.at[me],
            device_id=there, device_id_type=MESH))
        shares[-1].start()
    for k in range(1, devices):
        sender = (y + outer - k // inner) % outer * inner + (d + inner - k % inner) % inner
        pltpu.make_async_remote_copy(
            src_ref=xout, dst_ref=xin.at[sender], send_sem=xsend_sem.at[k], recv_sem=xrecv_sem.at[sender],
            device_id=partner, device_id_type=MESH).wait_recv()

    parts = xin[...]
    top = jnp.max(parts, axis=0)
    full = top + jnp.log(jnp.sum(jnp.exp(parts - top[None]), axis=0))
    positives = jnp.sum(parts, axis=0)[halves:halves + 1]
    total = jnp.sum(jnp.sum(full[:halves], axis=0, keepdims=True) - positives)
    mean_ref[0] = total / (devices * pairs)
    row = full[0:1]
    for h in range(1, halves):
        row = jnp.where(me // per_half == h, full[h:h + 1], row)
    row = pltpu.roll(row - own_row, (LANES - me % per_half * pairs) % LANES, 1)
    loss_ref[...] = row[:, :pairs]

    for send in sends + shares:
        send.wait_send()
    for i in range(1, chips):
        block_copy(me, relay_sem.at[i], partner).wait_send()


def solution(mesh):
    outer, inner = mesh.shape['data2'], mesh.shape['data']
    row_spec = P(('replica', 'data2', 'data'))
    tok_spec = P(('replica', 'data2', 'data'), None, None)
    mask_spec = P(('replica', 'data2', 'data'), None)

    def local_step(query_hidden, doc_hidden, w_proj, query_mask, doc_mask, temperature):
        pairs, qlen, hidden = query_hidden.shape
        dlen, width = doc_hidden.shape[1], w_proj.shape[1]
        devices, chips, tokens = outer * inner, outer * inner // CORES, pairs * qlen
        share_rows = -(-(devices * pairs // LANES + 1) // 4) * 4
        anywhere = pl.BlockSpec(memory_space=pltpu.HBM)
        vmem, dma = pltpu.VMEM, pltpu.SemaphoreType.DMA
        losses, mean_loss = pl.pallas_call(
            functools.partial(kernel, outer, inner, pairs, qlen, dlen),
            out_shape=(jax.ShapeDtypeStruct((1, pairs), jnp.float32), jax.ShapeDtypeStruct((1,), jnp.float32)),
            in_specs=[anywhere] * 5 + [pl.BlockSpec(memory_space=pltpu.SMEM)],
            out_specs=(pl.BlockSpec(memory_space=pltpu.VMEM), pl.BlockSpec(memory_space=pltpu.SMEM)),
            scratch_shapes=[
                vmem((tokens, hidden), jnp.bfloat16),
                vmem((pairs * dlen, hidden), jnp.bfloat16),
                vmem((hidden, width), jnp.bfloat16),
                vmem((pairs, qlen), jnp.int32),
                vmem((pairs, dlen), jnp.int32),
                vmem((devices, 2 * width, tokens), jnp.bfloat16),
                vmem((pairs * dlen, 2 * width), jnp.bfloat16),
                vmem((devices, pairs, tokens), jnp.float32),
                vmem((share_rows, LANES), jnp.float32),
                vmem((devices, share_rows, LANES), jnp.float32),
                dma((4,)), dma((DOC_CHUNKS,)), dma((chips,)), dma((chips,)), dma((devices,)),
                dma((devices,)), dma((devices,)),
            ],
            compiler_params=pltpu.CompilerParams(
                collective_id=0, has_side_effects=True, vmem_limit_bytes=67043328),
            name='late_interaction',
        )(query_hidden.reshape(tokens, hidden), doc_hidden.reshape(pairs * dlen, hidden), w_proj,
          query_mask, doc_mask, temperature.reshape(1))
        return losses.reshape(pairs), mean_loss

    return jax.shard_map(local_step, mesh=mesh,
                         in_specs=(tok_spec, tok_spec, P(None, None), mask_spec, mask_spec, P()),
                         out_specs=(row_spec, P('replica')), check_vma=False)
```

time: 197 us -> 48.6 us (0.25)
  blocking collectives: 73.2 us -> 0 us
  matrix products: 59.7 us -> 0 us
  Pallas kernels: 0 us -> 44.4 us
  waiting for transfers between devices: 30.6 us -> 0 us
  between operations: 16.7 us -> 3.05 us
  other arithmetic: 6.69 us -> 0 us
  starting transfers between devices: 3.4 us -> 0 us
  local copies, waits for them, and re-layouts: 4.49 us -> 1.11 us
    dot_general x34 -> x0, matrix products: 59.7 us -> none  [the longest x32 52.2 us: tile_scores(): jnp.einsum('qtc,jsc->qtjs', q_block, p_block, preferred_element_type=jnp....]
    pallas_call x0 -> x1, Pallas kernels: none -> 44.4 us  [local_step(): pl.pallas_call(functools.partial(kernel, outer, inner, pairs, qlen, dlen)...]
    psum x1 -> x0, blocking collectives: 44 us -> none  [local_step(): mean_loss = lax.psum(jnp.sum(losses), batch_axes) / total_batch]
    all_gather x1 -> x0, waiting for transfers between devices: 27.4 us -> none  [local_step(): q_all = lax.all_gather(q_all, 'data2', axis=0, tiled=True)]
    all_gather x1 -> x0, blocking collectives: 19.6 us -> none  [local_step(): q_all = lax.all_gather(q_vecs, 'data', axis=0, tiled=True)]
    all_to_all x1 -> x0, blocking collectives: 9.62 us -> none  [local_step(): column = lax.all_to_all(column, 'data', 1, 1, tiled=True)]
    reduce_sum x34 -> x0, other arithmetic: 4.01 us -> none  [the longest x32 2.66 us: tile_scores(): return jnp.sum(best_match, axis=1)]
    all_to_all x1 -> x0, starting transfers between devices: 3.34 us -> none  [local_step(): column = lax.all_to_all(column, 'data2', 0, 0, tiled=True)]
  transfers between devices with their start and end apart: 2 -> 0, of which waited for: 2 -> 0; matrix products, arithmetic and copies ran while one was open for 4% -> 0% of each run, Pallas kernels for 0% -> 0%
where the time goes in v1:
time: 48.6 us; the launch traced here: 48.5 us
  Pallas kernels  44.4 us (91%)
  between operations  3.05 us (6%)
  local copies, waits for them, and re-layouts  1.11 us (2%)
    pallas_call x1, Pallas kernels, local_step(): pl.pallas_call(functools.partial(kernel, outer, inner, pairs, qlen, dlen)...  44.4 us
    unnamed x1, local copies, waits for them, and re-layouts  1.11 us

profile of v1, /device:TPU:97, one launch (start us, length us, event | category | flops | bytes accessed | tf_op | source)
XLA Modules:
  0.0 48.5 jit_solution(12227337139219916293)
XLA Ops:
  1.3 44.4 %late_interaction.1 = (f32[1,8]{1,0:T(1,128)}, f32[1]{0:T(128)}) custom-call(bf16[256,1024]{1,0:T(8,128)(2,1)} %bitcast.6, bf16[4096,1024]{1,0:T(8,128)(2,1)} %bitcast.5, bf16[1024,128]{1,0:T(8,128)(2,1)} %w_hbm.1, s32[8,32]{1,0:T(8,128)} %qm_hbm.1, s32[8,512]{1,0:T(8,128)} %dm_hbm.1, f32[1]{0:T(128)} %bitcast.4.temp_ref), custom_call_target="tpu_custom_call" | custom-call | tf_op jit(solution)/shard_map/late_interaction/pallas_call | solution.py:193
  45.7 1.1 %copy.11 = f32[8]{0:T(128)} copy(f32[8]{0:T(128)} %bitcast.7) | data formatting | bytes 64
